TPU v7x, 32 devices: a whole 2x2x4 slice. The times are simulated.
32 devices in a mesh: shots: 2 (over y), rx: 4 (over z), ta: 2 (over x), af: 2 (over core).
Axes of the slice: x: 2, y: 2, z: 4, core: 2. Of those that a mesh axis runs over, the one named last changes fastest.
Arguments:
- traces: bfloat16 [4096, 512], P(('shots', 'rx'), ('ta', 'af')), parts along dimension 0, may hold values from -6 to 6
- slopes: int32 [512], replicated, may hold values from 0 to 1023
- offsets: int32 [4096], P('shots'), parts along dimension 0, may hold values from 1 to 4095
- live: int32 [4096], P('shots'), parts along dimension 0, may hold values 0 or 1
Outputs:
- stack: float32 [1024, 512], P(('shots', 'rx'), ('ta', 'af')), parts along dimension 0
- coherence: float32 [1024, 512], P(('shots', 'rx'), ('ta', 'af')), parts along dimension 0
- peak_values: float32 [1024], P(('shots', 'rx')), parts along dimension 0
There are 2 independent parts, one for each index of `shots`. A program takes and returns all parts, laid end to end along the dimension named above; an argument that names none is the same for every part. Nothing has to cross between parts.
Inputs may be any that keep to these rules, and one draw needn't show every extreme that they name: delays are below 64: (slopes * offsets) // 65536 < 64.
All inputs are finite; a program needn't handle non-finite values.
Results may differ from a plain program's by a relative error of at most 0.0003.
Values may be sent and summed in bfloat16 or wider, within the bound.
A program may use at most 64 MiB of HBM per device.

v0:
```python
import functools

import jax
import jax.numpy as jnp
from jax import lax
from jax.experimental import pallas as pl
from jax.experimental.pallas import tpu as pltpu
from jax.sharding import PartitionSpec as P

SPAN = 64
WIN = 16
PHASES = 16
MESH = pl.DeviceIdType.MESH
F32 = jnp.float32
BF16 = jnp.bfloat16


def window_sum(rows, width):
    reach = 1
    while reach < width:
        rows = rows[:-reach] + rows[reach:]
        reach *= 2
    return rows


def kernel(
    n_rx, n_ta, n_af, groups, halves,
    traces_ref, slopes_ref, offsets_ref, live_ref,
    stack_ref, coherence_ref, peak_ref,
    cols, halo, delays, long, parts, arrived, lead, lead_in, top, top_in,
    gather_send, gather_recv, halo_send, halo_recv,
    part_send, part_recv, lead_send, lead_recv, top_send, top_recv,
):
    blocks = n_ta * n_af
    members = n_rx // groups
    local_rows, block_len = traces_ref.shape
    half_rows = local_rows // halves
    group_slows = slopes_ref.shape[1] // groups
    own_slows = group_slows // members
    rx = lax.axis_index("rx")
    group, member = lax.div(rx, members), lax.rem(rx, members)
    other_rx = (groups - 1 - group) * members + member
    block = lax.axis_index("ta") * n_af + lax.axis_index("af")
    has_previous = block > 0
    has_next = block < blocks - 1

    def at_block(number):
        return {"ta": lax.div(number, n_af), "af": lax.rem(number, n_af)}

    previous = at_block(jnp.maximum(block - 1, 0))
    block_peers = [at_block(lax.rem(block + step, blocks)) for step in range(1, blocks)]
    member_peers = [lax.rem(member + step, members) for step in range(1, members)]

    peers = list(block_peers)
    for peer in member_peers:
        peer_rx = {"rx": group * members + peer}
        peers.append(peer_rx)
        if blocks > 1:
            peers += [peer_rx | block_peers[0], peer_rx | block_peers[-1]]
    if groups > 1:
        peers.append({"rx": other_rx})
    barrier = pltpu.get_barrier_semaphore()
    for peer in peers:
        pl.semaphore_signal(barrier, inc=1, device_id=peer, device_id_type=MESH)

    for half in range(halves):
        rows = traces_ref[half * half_rows : (half + 1) * half_rows, :]
        cols[half] = rows.astype(F32).T.astype(BF16)

    @pl.when(jnp.logical_not(has_next))
    def _():
        halo[...] = jnp.zeros_like(halo)
        lead_in[...] = jnp.zeros_like(lead_in)

    pl.semaphore_wait(barrier, len(peers))

    def gather(half):
        return pltpu.make_async_remote_copy(
            src_ref=cols.at[half], dst_ref=cols.at[halves + half],
            send_sem=gather_send.at[half], recv_sem=gather_recv.at[half],
            device_id={"rx": other_rx}, device_id_type=MESH,
        )

    def pass_halo(index):
        return pltpu.make_async_remote_copy(
            src_ref=cols.at[index, pl.ds(0, SPAN)], dst_ref=halo.at[index],
            send_sem=halo_send.at[index], recv_sem=halo_recv.at[index],
            device_id=previous, device_id_type=MESH,
        )

    @pl.when(has_previous)
    def _():
        for half in range(halves):
            pass_halo(half).start()

    if groups > 1:
        for half in range(halves):
            gather(half).start()

    slopes = slopes_ref[:, pl.ds(pl.multiple_of(group * group_slows, group_slows), group_slows)]
    slopes = slopes.astype(F32)
    for index in range(groups * halves):
        side, half = divmod(index, halves)
        start = (other_rx if side else rx) * local_rows + half * half_rows
        lanes = pl.ds(pl.multiple_of(start, half_rows), half_rows)
        offsets = offsets_ref[:, lanes].astype(F32)
        marked = jnp.where(live_ref[:, lanes] != 0, offsets, 65536.0)
        column = jnp.broadcast_to(marked, (128, half_rows)).T
        column = jnp.concatenate([column] * (-(-group_slows // 128)), axis=1)[:, :group_slows]
        delay = jnp.floor(column * slopes * (1.0 / 65536.0))
        delays[index] = jnp.where(column < 65536.0, delay, 127.0).astype(BF16)

    parts[...] = jnp.zeros_like(parts)
    kept = block_len + SPAN - PHASES

    def add_block(index, carry):
        if groups > 1:
            @pl.when(jnp.logical_and(index >= 1, index <= halves))
            def _():
                gather(index - 1).wait_recv()

                @pl.when(has_previous)
                def _():
                    pass_halo(index - 1 + halves).start()

        @pl.when(has_next)
        def _():
            pass_halo(index).wait_recv()

        long[0:block_len] = cols[index].astype(F32)
        long[block_len:] = halo[index].astype(F32)
        delay = delays[index]
        for phase in range(PHASES):
            samples = long[phase : phase + kept]
            squares = (samples * samples).astype(BF16)
            samples = samples.astype(BF16)
            left, right = [], []
            for lag in range(0, SPAN, PHASES):
                left.append(jnp.concatenate(
                    [samples[lag : lag + block_len], squares[lag : lag + block_len]], axis=0))
                right.append(jnp.where(delay == jnp.asarray(lag + phase, BF16),
                                       jnp.asarray(1, BF16), jnp.asarray(0, BF16)))
            product = jnp.dot(jnp.concatenate(left, axis=1), jnp.concatenate(right, axis=0),
                              preferred_element_type=F32)
            for part in range(members):
                parts[part] += product[:, part * own_slows : (part + 1) * own_slows]
        return carry

    lax.fori_loop(0, groups * halves, add_block, 0)

    for part in range(members):
        lead[part, 0:WIN] = parts[part, 0:WIN]
        lead[part, WIN:] = parts[part, block_len : block_len + WIN]

    def pass_lead(step):
        peer = lax.rem(member + step, members)
        return pltpu.make_async_remote_copy(
            src_ref=lead.at[peer], dst_ref=lead_in.at[step],
            send_sem=lead_send.at[step], recv_sem=lead_recv.at[step],
            device_id={"rx": group * members + peer} | previous, device_id_type=MESH,
        )

    @pl.when(has_previous)
    def _():
        for step in range(members):
            pass_lead(step).start()

    exchanges = []
    for step, peer in enumerate(member_peers):
        exchanges.append(pltpu.make_async_remote_copy(
            src_ref=parts.at[peer], dst_ref=arrived.at[step],
            send_sem=part_send.at[step], recv_sem=part_recv.at[step],
            device_id={"rx": group * members + peer}, device_id_type=MESH,
        ))
        exchanges[-1].start()
    total = parts[member]
    for step, exchange in enumerate(exchanges):
        exchange.wait_recv()
        total = total + arrived[step]

    stack, energy = total[:block_len], total[block_len:]
    stack_ref[...] = stack.T

    @pl.when(has_next)
    def _():
        for step in range(members):
            pass_lead(step).wait_recv()

    following = lead_in[0]
    for step in range(1, members):
        following = following + lead_in[step]
    long_stack = jnp.concatenate([stack, following[:WIN]], axis=0)
    long_energy = jnp.concatenate([energy, following[WIN:]], axis=0)
    power_sum = window_sum(long_stack * long_stack, WIN)[:block_len]
    energy_sum = window_sum(long_energy, WIN)[:block_len]
    coherence = power_sum / jnp.maximum(energy_sum, 1.0)
    peak = jnp.max(coherence, axis=0, keepdims=True)
    top[...] = peak
    tops = []
    for step, peer in enumerate(block_peers):
        tops.append(pltpu.make_async_remote_copy(
            src_ref=top, dst_ref=top_in.at[step],
            send_sem=top_send.at[step], recv_sem=top_recv.at[step],
            device_id=peer, device_id_type=MESH,
        ))
        tops[-1].start()
    coherence_ref[...] = coherence.T
    for step, copy in enumerate(tops):
        copy.wait_recv()
        peak = jnp.maximum(peak, top_in[step])
    peak_ref[...] = peak

    for copy in tops + exchanges:
        copy.wait_send()
    if groups > 1:
        for half in range(halves):
            gather(half).wait_send()

    @pl.when(has_previous)
    def _():
        for step in range(members):
            pass_lead(step).wait_send()
        for index in range(groups * halves):
            pass_halo(index).wait_send()


def solution(mesh):
    n_rx, n_ta, n_af = (mesh.shape[name] for name in ("rx", "ta", "af"))
    groups = 2 if n_rx % 2 == 0 else 1
    members = n_rx // groups

    def on_device(traces, slopes, offsets, live):
        local_rows, block_len = traces.shape
        halves = 2 if local_rows % 512 == 0 else 1
        half_rows = local_rows // halves
        group_slows = slopes.shape[0] // groups
        own_slows = group_slows // members
        sides = groups * halves
        dma = pltpu.SemaphoreType.DMA
        blocks = n_ta * n_af
        vmem = pl.BlockSpec(memory_space=pltpu.VMEM)
        stack, coherence, peak = pl.pallas_call(
            functools.partial(kernel, n_rx, n_ta, n_af, groups, halves),
            out_shape=(
                jax.ShapeDtypeStruct((own_slows, block_len), F32),
                jax.ShapeDtypeStruct((own_slows, block_len), F32),
                jax.ShapeDtypeStruct((1, own_slows), F32),
            ),
            in_specs=[vmem] * 4,
            out_specs=(vmem,) * 3,
            scratch_shapes=[
                pltpu.VMEM((sides, block_len, half_rows), BF16),
                pltpu.VMEM((sides, SPAN, half_rows), BF16),
                pltpu.VMEM((sides, half_rows, group_slows), BF16),
                pltpu.VMEM((block_len + SPAN, half_rows), F32),
                pltpu.VMEM((members, 2 * block_len, own_slows), F32),
                pltpu.VMEM((max(members - 1, 1), 2 * block_len, own_slows), F32),
                pltpu.VMEM((members, 2 * WIN, own_slows), F32),
                pltpu.VMEM((members, 2 * WIN, own_slows), F32),
                pltpu.VMEM((1, own_slows), F32),
                pltpu.VMEM((max(blocks - 1, 1), 1, own_slows), F32),
                dma((halves,)), dma((halves,)),
                dma((sides,)), dma((sides,)),
                dma((max(members - 1, 1),)), dma((max(members - 1, 1),)),
                dma((members,)), dma((members,)),
                dma((max(blocks - 1, 1),)), dma((max(blocks - 1, 1),)),
            ],
            compiler_params=pltpu.CompilerParams(collective_id=0, has_side_effects=True),
            name="slant_stack",
        )(traces, slopes[None], offsets[None], live[None])
        return stack, coherence, peak[0]

    return jax.shard_map(
        on_device,
        mesh=mesh,
        in_specs=(P(("shots", "rx"), ("ta", "af")), P(), P("shots"), P("shots")),
        out_specs=(
            P(("shots", "rx"), ("ta", "af")),
            P(("shots", "rx"), ("ta", "af")),
            P(("shots", "rx")),
        ),
        check_vma=False,
    )
```

profile of v0, /device:TPU:12, one launch (start us, length us, event | category | flops | bytes accessed | tf_op | source)
XLA Modules:
  0.0 29.2 jit_solution(5355438301325331137)
XLA Ops:
  0.6 25.9 %slant_stack.1 = (f32[128,128]{1,0:T(8,128)}, f32[128,128]{1,0:T(8,128)}, f32[1,128]{1,0:T(1,128)}) custom-call(bf16[512,128]{1,0:T(8,128)(2,1)} %traces_ref.1, s32[1,512]{1,0:T(1,128)} %bitcast.6, s32[1,2048]{1,0:T(1,128)} %bitcast.4, s32[1,2048]{1,0:T(1,128)} %bitcast.5), custom_call_target="tpu_custom_call" | custom-call | tf_op jit(solution)/shard_map/slant_stack/pallas_call | solution.py:242
  26.5 0.0 copy-start
  26.5 1.5 %copy.10 = f32[128,128]{1,0:T(8,128)} copy(f32[128,128]{1,0:T(8,128)} %get-tuple-element.12) | data formatting | bytes 131072
  28.0 0.0 copy-done
  28.0 0.0 copy-start.1
  28.0 0.6 %copy.11 = f32[128,128]{1,0:T(8,128)} copy(f32[128,128]{1,0:T(8,128)S(1)} %copy-done) | data formatting | bytes 131072
  28.7 0.0 copy-done.1
  28.7 0.5 %copy.12 = f32[128]{0:T(128)} copy(f32[128]{0:T(128)S(1)} %bitcast.7) | data formatting | bytes 1024
Async XLA Ops:
  26.5 1.5 %copy-start = (f32[128,128]{1,0:T(8,128)S(1)}, f32[128,128]{1,0:T(8,128)}, u32[]{:S(2)}) copy-start(f32[128,128]{1,0:T(8,128)} %get-tuple-element.13) | copy-start | bytes 196612
  28.0 0.6 %copy-start.1 = (f32[1,128]{1,0:T(1,128)S(1)}, f32[1,128]{1,0:T(1,128)}, u32[]{:S(2)}) copy-start(f32[1,128]{1,0:T(1,128)} %get-tuple-element.8) | copy-start | bytes 1540
where the time goes:
time: 29.4 us; the launch traced here: 29.2 us
  Pallas kernels  25.9 us (88%)
  local copies, waits for them, and re-layouts  2.65 us (9%)
  between operations  0.65 us (2%)
    pallas_call x1, Pallas kernels, on_device(): pl.pallas_call(functools.partial(kernel, n_rx, n_ta, n_af, groups, halves...  25.9 us
    unnamed x7, local copies, waits for them, and re-layouts  2.65 us

commit v1 on v0

v1 whole, which is shorter than its diff:
```python
import functools

import jax
import jax.numpy as jnp
from jax import lax
from jax.experimental import pallas as pl
from jax.experimental.pallas import tpu as pltpu
from jax.sharding import PartitionSpec as P

SPAN = 64
WIN = 16
STEP = 8
EDGE = SPAN + WIN
MESH = pl.DeviceIdType.MESH
F32 = jnp.float32
BF16 = jnp.bfloat16


def window_sum(rows, width):
    reach = 1
    while reach < width:
        rows = rows[:-reach] + rows[reach:]
        reach *= 2
    return rows


def kernel(
    n_rx, n_ta, n_af, subs, pair,
    traces_hbm, slopes_hbm, offsets_hbm, live_hbm,
    stack_ref, coherence_ref, peak_ref,
    slopes_ref, offsets_ref, live_ref,
    held, delays, long, left, total, edge_in, top, top_in,
    in_sem, small_sem, gather_recv, right_send, left_send,
    edge_send, edge_recv, top_send, top_recv,
):
    blocks = n_ta * n_af
    sub_rows, block_len = held.shape[2:]
    own_slows = delays.shape[2]
    tall = block_len + STEP
    rx = lax.axis_index("rx")
    block = lax.axis_index("ta") * n_af + lax.axis_index("af")
    has_previous = block > 0
    has_next = block < blocks - 1
    has_left = rx > 0
    has_right = rx < n_rx - 1

    def at_block(number):
        return {"ta": lax.div(number, n_af), "af": lax.rem(number, n_af)}

    previous = at_block(jnp.maximum(block - 1, 0))
    block_peers = [at_block(lax.rem(block + step, blocks)) for step in range(1, blocks)]

    barrier = pltpu.get_barrier_semaphore()

    @pl.when(has_left)
    def _():
        pl.semaphore_signal(barrier, inc=1, device_id={"rx": rx - 1}, device_id_type=MESH)

    @pl.when(has_right)
    def _():
        pl.semaphore_signal(barrier, inc=1, device_id={"rx": rx + 1}, device_id_type=MESH)

    for peer in block_peers:
        pl.semaphore_signal(barrier, inc=1, device_id=peer, device_id_type=MESH)

    small = [
        pltpu.make_async_copy(source, target, small_sem.at[index])
        for index, (source, target) in enumerate(
            [(slopes_hbm, slopes_ref), (offsets_hbm, offsets_ref), (live_hbm, live_ref)])
    ]
    own = [
        pltpu.make_async_copy(
            traces_hbm.at[pl.ds(sub * sub_rows, sub_rows)], held.at[rx, sub], in_sem.at[sub])
        for sub in range(subs)
    ]
    for copy in small + own:
        copy.start()

    def to_right(source, sub):
        return pltpu.make_async_remote_copy(
            src_ref=held.at[source, sub], dst_ref=held.at[source, sub],
            send_sem=right_send.at[source, sub], recv_sem=gather_recv.at[source, sub],
            device_id={"rx": jnp.minimum(rx + 1, n_rx - 1)}, device_id_type=MESH,
        )

    def to_left(source, sub):
        return pltpu.make_async_remote_copy(
            src_ref=held.at[source, sub], dst_ref=held.at[source, sub],
            send_sem=left_send.at[source, sub], recv_sem=gather_recv.at[source, sub],
            device_id={"rx": jnp.maximum(rx - 1, 0)}, device_id_type=MESH,
        )

    total[...] = jnp.zeros_like(total)
    long[0:STEP] = jnp.zeros((STEP, sub_rows), F32)
    long[block_len + STEP:] = jnp.zeros((STEP, sub_rows), F32)

    @pl.when(jnp.logical_not(has_next))
    def _():
        edge_in[...] = jnp.zeros_like(edge_in)

    for copy in small:
        copy.wait()

    near = jnp.where(has_left, 1, 0) + jnp.where(has_right, 1, 0)
    pl.semaphore_wait(barrier, near + blocks - 1)
    for sub in range(subs):
        own[sub].wait()

        @pl.when(has_right)
        def _():
            to_right(rx, sub).start()

        @pl.when(has_left)
        def _():
            to_left(rx, sub).start()

    slopes = slopes_ref[pl.ds(rx, 1), :].astype(F32)

    def set_delays(index, carry):
        lanes = pl.ds(pl.multiple_of(index * sub_rows, sub_rows), sub_rows)
        offsets = offsets_ref[:, lanes].astype(F32)
        marked = jnp.where(live_ref[:, lanes] != 0, offsets, 65536.0)
        column = jnp.broadcast_to(marked, (128, sub_rows)).T
        column = jnp.concatenate([column] * (-(-own_slows // 128)), axis=1)[:, :own_slows]
        delay = jnp.floor(column * slopes * (1.0 / 65536.0))
        delays[index] = jnp.where(column < 65536.0, delay, 127.0).astype(BF16)
        return carry

    lax.fori_loop(0, n_rx * subs, set_delays, 0)

    both = jnp.minimum(rx, n_rx - 1 - rx)

    def item_at(number):
        ahead = number - subs
        late = ahead - 2 * subs * both
        paired = late < 0
        spot = jnp.maximum(ahead, 0)
        tail = jnp.maximum(late, 0)
        distance = jnp.where(paired, lax.div(spot, 2 * subs), both + lax.div(tail, subs)) + 1
        sub = jnp.where(paired, lax.div(lax.rem(spot, 2 * subs), 2), lax.rem(tail, subs))
        leftward = jnp.where(paired, 1 - lax.rem(spot, 2), jnp.where(rx > n_rx - 1 - rx, 1, 0))
        distance = jnp.where(leftward == 1, -distance, distance)
        mine = number < subs
        return jnp.where(mine, rx, rx + distance), jnp.where(mine, number, sub)

    def exchange(step):
        distance = lax.div(step, subs) + 1
        sub = lax.rem(step, subs)
        before = jnp.maximum(rx - distance, 0)
        after = jnp.minimum(rx + distance, n_rx - 1)

        @pl.when(rx - distance >= 0)
        def _():
            to_right(before, sub).wait_recv()

            @pl.when(has_right)
            def _():
                to_right(before, sub).start()

        @pl.when(rx + distance < n_rx)
        def _():
            to_left(after, sub).wait_recv()

            @pl.when(has_left)
            def _():
                to_left(after, sub).start()

    def add_item(number, carry):
        @pl.when(number >= subs)
        def _():
            exchange(number - subs)

        source, sub = item_at(number)
        long[STEP:STEP + block_len] = held[source, sub].astype(F32).T
        delay = delays[source * subs + sub]
        for lag in range(STEP):
            samples = long[lag:lag + tall]
            left[:, lag * sub_rows:(lag + 1) * sub_rows] = jnp.concatenate(
                [samples, samples * samples], axis=0).astype(BF16)
        for first in range(0, SPAN // STEP, pair):
            right = [
                jnp.concatenate([
                    jnp.where(delay == jnp.asarray(STEP * (first + turn) + lag, BF16),
                              jnp.asarray(1, BF16), jnp.asarray(0, BF16))
                    for turn in range(pair)], axis=1)
                for lag in range(STEP)
            ]
            product = jnp.dot(left[...], jnp.concatenate(right, axis=0),
                              preferred_element_type=F32)
            for turn in range(pair):
                top_row = SPAN - STEP * (first + turn + 1)
                lanes = slice(turn * own_slows, (turn + 1) * own_slows)
                total[0, top_row:top_row + tall] += product[:tall, lanes]
                total[1, top_row:top_row + tall] += product[tall:, lanes]
        return carry

    lax.fori_loop(0, n_rx * subs, add_item, 0)

    pass_edge = pltpu.make_async_remote_copy(
        src_ref=total.at[:, pl.ds(0, EDGE)], dst_ref=edge_in,
        send_sem=edge_send, recv_sem=edge_recv,
        device_id=previous, device_id_type=MESH,
    )

    @pl.when(has_previous)
    def _():
        pass_edge.start()

    @pl.when(has_next)
    def _():
        pass_edge.wait_recv()

    near_rows = block_len - SPAN

    def whole(kind):
        return jnp.concatenate([
            total[kind, SPAN:SPAN + near_rows],
            total[kind, SPAN + near_rows:] + edge_in[kind, 0:SPAN],
            edge_in[kind, SPAN:],
        ], axis=0)

    stack, energy = whole(0), whole(1)
    power_sum = window_sum(stack * stack, WIN)[:block_len]
    energy_sum = window_sum(energy, WIN)[:block_len]
    coherence = power_sum / jnp.maximum(energy_sum, 1.0)
    peak = jnp.max(coherence, axis=0, keepdims=True)
    top[...] = peak
    tops = []
    for step, peer in enumerate(block_peers):
        tops.append(pltpu.make_async_remote_copy(
            src_ref=top, dst_ref=top_in.at[step],
            send_sem=top_send.at[step], recv_sem=top_recv.at[step],
            device_id=peer, device_id_type=MESH,
        ))
        tops[-1].start()
    stack_ref[...] = stack[:block_len].T
    coherence_ref[...] = coherence.T

    for source in range(n_rx):
        for sub in range(subs):
            @pl.when(jnp.logical_and(has_right, source <= rx))
            def _():
                to_right(source, sub).wait_send()

            @pl.when(jnp.logical_and(has_left, source >= rx))
            def _():
                to_left(source, sub).wait_send()

    @pl.when(has_previous)
    def _():
        pass_edge.wait_send()

    for step, copy in enumerate(tops):
        copy.wait_recv()
        peak = jnp.maximum(peak, top_in[step])
    peak_ref[...] = peak
    for copy in tops:
        copy.wait_send()


def emit(stack_ref, coherence_ref, peak_ref, stack_hbm, coherence_hbm, peak_hbm, sem):
    copies = [
        pltpu.make_async_copy(source, target, sem.at[index])
        for index, (source, target) in enumerate(
            [(stack_ref, stack_hbm), (coherence_ref, coherence_hbm), (peak_ref, peak_hbm)])
    ]
    for copy in copies:
        copy.start()
    for copy in copies:
        copy.wait()


def solution(mesh):
    n_rx, n_ta, n_af = (mesh.shape[name] for name in ("rx", "ta", "af"))

    def on_device(traces, slopes, offsets, live):
        local_rows, block_len = traces.shape
        subs = 2 if local_rows % 512 == 0 else 1
        sub_rows = local_rows // subs
        own_slows = slopes.shape[0] // n_rx
        pair = min(max(256 // own_slows, 1), SPAN // STEP)
        items = n_rx * subs
        blocks = n_ta * n_af
        tall = block_len + STEP
        dma = pltpu.SemaphoreType.DMA
        vmem = pl.BlockSpec(memory_space=pltpu.VMEM)
        anywhere = pl.BlockSpec(memory_space=pl.ANY)
        shapes = (
            jax.ShapeDtypeStruct((own_slows, block_len), F32),
            jax.ShapeDtypeStruct((own_slows, block_len), F32),
            jax.ShapeDtypeStruct((1, own_slows), F32),
        )
        results = pl.pallas_call(
            functools.partial(kernel, n_rx, n_ta, n_af, subs, pair),
            out_shape=shapes,
            in_specs=[anywhere] * 4,
            out_specs=(vmem,) * 3,
            scratch_shapes=[
                pltpu.VMEM((n_rx, own_slows), jnp.int32),
                pltpu.VMEM((1, n_rx * local_rows), jnp.int32),
                pltpu.VMEM((1, n_rx * local_rows), jnp.int32),
                pltpu.VMEM((n_rx, subs, sub_rows, block_len), BF16),
                pltpu.VMEM((items, sub_rows, own_slows), BF16),
                pltpu.VMEM((block_len + 2 * STEP, sub_rows), F32),
                pltpu.VMEM((2 * tall, STEP * sub_rows), BF16),
                pltpu.VMEM((2, block_len + SPAN, own_slows), F32),
                pltpu.VMEM((2, EDGE, own_slows), F32),
                pltpu.VMEM((1, own_slows), F32),
                pltpu.VMEM((max(blocks - 1, 1), 1, own_slows), F32),
                dma((subs,)), dma((3,)), dma((n_rx, subs)), dma((n_rx, subs)), dma((n_rx, subs)),
                dma, dma,
                dma((max(blocks - 1, 1),)), dma((max(blocks - 1, 1),)),
            ],
            compiler_params=pltpu.CompilerParams(collective_id=0, has_side_effects=True),
            name="slant_stack",
        )(traces, slopes.reshape(n_rx, own_slows), offsets[None], live[None])
        stack, coherence, peak = pl.pallas_call(
            emit,
            out_shape=shapes,
            in_specs=[vmem] * 3,
            out_specs=(anywhere,) * 3,
            scratch_shapes=[dma((3,))],
            name="emit",
        )(*results)
        return stack, coherence, peak[0]

    return jax.shard_map(
        on_device,
        mesh=mesh,
        in_specs=(P(("shots", "rx"), ("ta", "af")), P(), P("shots"), P("shots")),
        out_specs=(
            P(("shots", "rx"), ("ta", "af")),
            P(("shots", "rx"), ("ta", "af")),
            P(("shots", "rx")),
        ),
        check_vma=False,
    )
```

time: 29.4 us -> 25.7 us (0.87)
  the two profiles are of different devices: /device:TPU:12 before, /device:TPU:0 now
where the time goes in v1:
time: 25.7 us; the launch traced here: 25.5 us
  Pallas kernels  24.9 us (97%)
  between operations  0.64 us (2%)
    pallas_call x1, Pallas kernels, on_device(): pl.pallas_call(functools.partial(kernel, n_rx, n_ta, n_af, subs, pair), o...  23.3 us
    pallas_call x1, Pallas kernels, on_device(): pl.pallas_call(emit, out_shape=shapes, in_specs=[vmem] * 3, out_specs=(an...  1.55 us

profile of v1, /device:TPU:0, one launch (start us, length us, event | category | flops | bytes accessed | tf_op | source)
XLA Modules:
  0.0 25.5 jit_solution(12188807343432542628)
XLA Ops:
  0.6 23.3 %slant_stack.1 = (f32[128,128]{1,0:T(8,128)}, f32[128,128]{1,0:T(8,128)}, f32[1,128]{1,0:T(1,128)}) custom-call(bf16[512,128]{1,0:T(8,128)(2,1)} %traces_hbm.1, s32[4,128]{1,0:T(4,128)} %bitcast.6, s32[1,2048]{1,0:T(1,128)} %bitcast.4, s32[1,2048]{1,0:T(1,128)} %bitcast.5), custom_call_target="tpu_custom_call" | custom-call | tf_op jit(solution)/shard_map/slant_stack/pallas_call | solution.py:293
  23.9 1.6 %emit.1 = (f32[128,128]{1,0:T(8,128)}, f32[128,128]{1,0:T(8,128)}, f32[1,128]{1,0:T(1,128)}) custom-call(f32[128,128]{1,0:T(8,128)} %get-tuple-element.9.stack_ref, f32[128,128]{1,0:T(8,128)} %get-tuple-element.10.coherence_ref, f32[1,128]{1,0:T(1,128)} %get-tuple-element.11.peak_ref), custom_call_target="tpu_custom_call" | custom-call | tf_op jit(solution)/shard_map/emit/pallas_call | solution.py:317

commit v2 on v1

--- a/solution.py
+++ b/solution.py
@@ -11,6 +11,7 @@
 WIN = 16
 STEP = 8
 EDGE = SPAN + WIN
+FAR = 3
 MESH = pl.DeviceIdType.MESH
 F32 = jnp.float32
 BF16 = jnp.bfloat16
@@ -29,13 +30,13 @@
     traces_hbm, slopes_hbm, offsets_hbm, live_hbm,
     stack_ref, coherence_ref, peak_ref,
     slopes_ref, offsets_ref, live_ref,
-    held, delays, long, left, total, edge_in, top, top_in,
-    in_sem, small_sem, gather_recv, right_send, left_send,
+    held, delays, coming, long, left, total, edge_in, top, top_in,
+    in_sem, small_sem, gather_recv, right_send, left_send, far_send, far_ready,
     edge_send, edge_recv, top_send, top_recv,
 ):
     blocks = n_ta * n_af
     sub_rows, block_len = held.shape[2:]
-    own_slows = delays.shape[2]
+    own_slows = delays.shape[1]
     tall = block_len + STEP
     rx = lax.axis_index("rx")
     block = lax.axis_index("ta") * n_af + lax.axis_index("af")
@@ -62,6 +63,13 @@
 
     for peer in block_peers:
         pl.semaphore_signal(barrier, inc=1, device_id=peer, device_id_type=MESH)
+
+    for reach in range(FAR, n_rx):
+        @pl.when(rx + reach < n_rx)
+        def _():
+            pl.semaphore_signal(
+                barrier, inc=1, device_id={"rx": jnp.minimum(rx + reach, n_rx - 1)},
+                device_id_type=MESH)
 
     small = [
         pltpu.make_async_copy(source, target, small_sem.at[index])
@@ -90,6 +98,13 @@
             device_id={"rx": jnp.maximum(rx - 1, 0)}, device_id_type=MESH,
         )
 
+    def to_far(target, sub):
+        return pltpu.make_async_remote_copy(
+            src_ref=held.at[rx, sub], dst_ref=held.at[rx, sub],
+            send_sem=far_send.at[target, sub], recv_sem=gather_recv.at[rx, sub],
+            device_id={"rx": target}, device_id_type=MESH,
+        )
+
     total[...] = jnp.zeros_like(total)
     long[0:STEP] = jnp.zeros((STEP, sub_rows), F32)
     long[block_len + STEP:] = jnp.zeros((STEP, sub_rows), F32)
@@ -102,7 +117,7 @@
         copy.wait()
 
     near = jnp.where(has_left, 1, 0) + jnp.where(has_right, 1, 0)
-    pl.semaphore_wait(barrier, near + blocks - 1)
+    pl.semaphore_wait(barrier, near + blocks - 1 + jnp.maximum(rx - FAR + 1, 0))
     for sub in range(subs):
         own[sub].wait()
 
@@ -114,19 +129,25 @@
         def _():
             to_left(rx, sub).start()
 
+        for reach in range(FAR, n_rx):
+            @pl.when(rx >= reach)
+            def _():
+                target = jnp.maximum(rx - reach, 0)
+                to_far(target, sub).start()
+                if sub == 0:
+                    pl.semaphore_signal(
+                        far_ready, inc=1, device_id={"rx": target}, device_id_type=MESH)
+
     slopes = slopes_ref[pl.ds(rx, 1), :].astype(F32)
 
-    def set_delays(index, carry):
-        lanes = pl.ds(pl.multiple_of(index * sub_rows, sub_rows), sub_rows)
+    def delays_of(source, sub):
+        lanes = pl.ds(pl.multiple_of((source * subs + sub) * sub_rows, sub_rows), sub_rows)
         offsets = offsets_ref[:, lanes].astype(F32)
         marked = jnp.where(live_ref[:, lanes] != 0, offsets, 65536.0)
         column = jnp.broadcast_to(marked, (128, sub_rows)).T
         column = jnp.concatenate([column] * (-(-own_slows // 128)), axis=1)[:, :own_slows]
         delay = jnp.floor(column * slopes * (1.0 / 65536.0))
-        delays[index] = jnp.where(column < 65536.0, delay, 127.0).astype(BF16)
-        return carry
-
-    lax.fori_loop(0, n_rx * subs, set_delays, 0)
+        return jnp.where(column < 65536.0, delay, 127.0).astype(BF16)
 
     both = jnp.minimum(rx, n_rx - 1 - rx)
 
@@ -136,20 +157,21 @@
         paired = late < 0
         spot = jnp.maximum(ahead, 0)
         tail = jnp.maximum(late, 0)
-        distance = jnp.where(paired, lax.div(spot, 2 * subs), both + lax.div(tail, subs)) + 1
+        place = lax.div(tail, subs)
+        away = jnp.where(
+            both == 0, jnp.where(place == 0, 0, n_rx - 1 - place), both + place)
+        distance = jnp.where(paired, lax.div(spot, 2 * subs), away) + 1
         sub = jnp.where(paired, lax.div(lax.rem(spot, 2 * subs), 2), lax.rem(tail, subs))
         leftward = jnp.where(paired, 1 - lax.rem(spot, 2), jnp.where(rx > n_rx - 1 - rx, 1, 0))
         distance = jnp.where(leftward == 1, -distance, distance)
         mine = number < subs
         return jnp.where(mine, rx, rx + distance), jnp.where(mine, number, sub)
 
-    def exchange(step):
-        distance = lax.div(step, subs) + 1
-        sub = lax.rem(step, subs)
-        before = jnp.maximum(rx - distance, 0)
-        after = jnp.minimum(rx + distance, n_rx - 1)
-
-        @pl.when(rx - distance >= 0)
+    def exchange(sub):
+        before = jnp.maximum(rx - 1, 0)
+        after = jnp.minimum(rx + 1, n_rx - 1)
+
+        @pl.when(has_left)
         def _():
             to_right(before, sub).wait_recv()
 
@@ -157,7 +179,7 @@
             def _():
                 to_right(before, sub).start()
 
-        @pl.when(rx + distance < n_rx)
+        @pl.when(has_right)
         def _():
             to_left(after, sub).wait_recv()
 
@@ -165,14 +187,36 @@
             def _():
                 to_left(after, sub).start()
 
+    far_count = jnp.maximum(n_rx - FAR - rx, 0)
+
     def add_item(number, carry):
-        @pl.when(number >= subs)
-        def _():
-            exchange(number - subs)
-
         source, sub = item_at(number)
+
+        pace = jnp.where(both > 0, 2, 1)
+        turn = lax.div(number - subs, pace)
+
+        @pl.when(jnp.logical_and(
+            number >= subs,
+            jnp.logical_and(turn < subs, lax.rem(number - subs, pace) == 0)))
+        def _():
+            exchange(turn)
+
+        @pl.when(jnp.abs(source - rx) > 1)
+        def _():
+            to_right(source, sub).wait_recv()
+
+        @pl.when(jnp.logical_and(number == 1, far_count > 0))
+        def _():
+            pl.semaphore_wait(far_ready, far_count)
+            for reach in range(FAR, n_rx):
+                @pl.when(rx + reach < n_rx)
+                def _():
+                    for far_sub in range(subs):
+                        to_far(jnp.minimum(rx + reach, n_rx - 1), far_sub).start()
+
+        delays[...] = coming[...]
         long[STEP:STEP + block_len] = held[source, sub].astype(F32).T
-        delay = delays[source * subs + sub]
+        delay = delays[...]
         for lag in range(STEP):
             samples = long[lag:lag + tall]
             left[:, lag * sub_rows:(lag + 1) * sub_rows] = jnp.concatenate(
@@ -192,7 +236,10 @@
                 lanes = slice(turn * own_slows, (turn + 1) * own_slows)
                 total[0, top_row:top_row + tall] += product[:tall, lanes]
                 total[1, top_row:top_row + tall] += product[tall:, lanes]
+        coming[...] = delays_of(*item_at(jnp.minimum(number + 1, n_rx * subs - 1)))
         return carry
+
+    coming[...] = delays_of(rx, 0)
 
     lax.fori_loop(0, n_rx * subs, add_item, 0)
 
@@ -236,15 +283,28 @@
     stack_ref[...] = stack[:block_len].T
     coherence_ref[...] = coherence.T
 
-    for source in range(n_rx):
-        for sub in range(subs):
-            @pl.when(jnp.logical_and(has_right, source <= rx))
-            def _():
-                to_right(source, sub).wait_send()
-
-            @pl.when(jnp.logical_and(has_left, source >= rx))
-            def _():
-                to_left(source, sub).wait_send()
+    for sub in range(subs):
+        @pl.when(has_right)
+        def _():
+            to_right(rx, sub).wait_send()
+
+        @pl.when(has_left)
+        def _():
+            to_left(rx, sub).wait_send()
+
+        @pl.when(jnp.logical_and(has_left, has_right))
+        def _():
+            to_right(jnp.maximum(rx - 1, 0), sub).wait_send()
+            to_left(jnp.minimum(rx + 1, n_rx - 1), sub).wait_send()
+
+        for reach in range(FAR, n_rx):
+            @pl.when(rx >= reach)
+            def _():
+                to_far(jnp.maximum(rx - reach, 0), sub).wait_send()
+
+            @pl.when(rx + reach < n_rx)
+            def _():
+                to_far(jnp.minimum(rx + reach, n_rx - 1), sub).wait_send()
 
     @pl.when(has_previous)
     def _():
@@ -279,7 +339,6 @@
         sub_rows = local_rows // subs
         own_slows = slopes.shape[0] // n_rx
         pair = min(max(256 // own_slows, 1), SPAN // STEP)
-        items = n_rx * subs
         blocks = n_ta * n_af
         tall = block_len + STEP
         dma = pltpu.SemaphoreType.DMA
@@ -293,14 +352,15 @@
         results = pl.pallas_call(
             functools.partial(kernel, n_rx, n_ta, n_af, subs, pair),
             out_shape=shapes,
-            in_specs=[anywhere] * 4,
+            in_specs=[pl.BlockSpec(memory_space=pltpu.HBM)] * 4,
             out_specs=(vmem,) * 3,
             scratch_shapes=[
                 pltpu.VMEM((n_rx, own_slows), jnp.int32),
                 pltpu.VMEM((1, n_rx * local_rows), jnp.int32),
                 pltpu.VMEM((1, n_rx * local_rows), jnp.int32),
                 pltpu.VMEM((n_rx, subs, sub_rows, block_len), BF16),
-                pltpu.VMEM((items, sub_rows, own_slows), BF16),
+                pltpu.VMEM((sub_rows, own_slows), BF16),
+                pltpu.VMEM((sub_rows, own_slows), BF16),
                 pltpu.VMEM((block_len + 2 * STEP, sub_rows), F32),
                 pltpu.VMEM((2 * tall, STEP * sub_rows), BF16),
                 pltpu.VMEM((2, block_len + SPAN, own_slows), F32),
@@ -308,18 +368,20 @@
                 pltpu.VMEM((1, own_slows), F32),
                 pltpu.VMEM((max(blocks - 1, 1), 1, own_slows), F32),
                 dma((subs,)), dma((3,)), dma((n_rx, subs)), dma((n_rx, subs)), dma((n_rx, subs)),
+                dma((n_rx, subs)), pltpu.SemaphoreType.REGULAR,
                 dma, dma,
                 dma((max(blocks - 1, 1),)), dma((max(blocks - 1, 1),)),
             ],
-            compiler_params=pltpu.CompilerParams(collective_id=0, has_side_effects=True),
+            compiler_params=pltpu.CompilerParams(collective_id=0, has_side_effects=True, vmem_limit_bytes=16777216),
             name="slant_stack",
-        )(traces, slopes.reshape(n_rx, own_slows), offsets[None], live[None])
+        )(*[pltpu.with_memory_space_constraint(a, pltpu.HBM) for a in (traces, slopes.reshape(n_rx, own_slows), offsets[None], live[None])])
         stack, coherence, peak = pl.pallas_call(
             emit,
             out_shape=shapes,
             in_specs=[vmem] * 3,
             out_specs=(anywhere,) * 3,
             scratch_shapes=[dma((3,))],
+            compiler_params=pltpu.CompilerParams(vmem_limit_bytes=4194304),
             name="emit",
         )(*results)
         return stack, coherence, peak[0]

time: 25.7 us -> 23.1 us (0.90)
  Pallas kernels: 24.9 us -> 22.3 us
    pallas_call x1, Pallas kernels: 23.3 us -> 21.6 us  [on_device(): pl.pallas_call(functools.partial(kernel, n_rx, n_ta, n_af, subs, pair), o...]
    pallas_call x1, Pallas kernels: 1.55 us -> 0.68 us  [on_device(): pl.pallas_call(emit, out_shape=shapes, in_specs=[vmem] * 3, out_specs=(an...]
where the time goes in v2:
time: 23.1 us; the launch traced here: 22.9 us
  Pallas kernels  22.3 us (97%)
  between operations  0.64 us (3%)
    pallas_call x1, Pallas kernels, on_device(): pl.pallas_call(functools.partial(kernel, n_rx, n_ta, n_af, subs, pair), o...  21.6 us
    pallas_call x1, Pallas kernels, on_device(): pl.pallas_call(emit, out_shape=shapes, in_specs=[vmem] * 3, out_specs=(an...  0.68 us

profile of v2, /device:TPU:0, one launch (start us, length us, event | category | flops | bytes accessed | tf_op | source)
XLA Modules:
  0.0 22.9 jit_solution(9385163541404006262)
XLA Ops:
  0.6 21.6 %slant_stack.1 = (f32[128,128]{1,0:T(8,128)S(1)}, f32[128,128]{1,0:T(8,128)S(1)}, f32[1,128]{1,0:T(1,128)S(1)}) custom-call(bf16[512,128]{1,0:T(8,128)(2,1)} %traces_hbm.1, s32[4,128]{1,0:T(4,128)} %bitcast.6, s32[1,2048]{1,0:T(1,128)} %bitcast.4, s32[1,2048]{1,0:T(1,128)} %bitcast.5), custom_call_target="tpu_custom_call" | custom-call | tf_op jit(solution)/shard_map/slant_stack/pallas_call | solution.py:352
  22.2 0.7 %emit.1 = (f32[128,128]{1,0:T(8,128)}, f32[128,128]{1,0:T(8,128)}, f32[1,128]{1,0:T(1,128)}) custom-call(f32[128,128]{1,0:T(8,128)S(1)} %get-tuple-element.9.stack_ref, f32[128,128]{1,0:T(8,128)S(1)} %get-tuple-element.10.coherence_ref, f32[1,128]{1,0:T(1,128)S(1)} %get-tuple-element.11.peak_ref), custom_call_target="tpu_custom_call" | custom-call | tf_op jit(solution)/shard_map/emit/pallas_call | solution.py:378

commit v3 on v2

--- a/solution.py
+++ b/solution.py
@@ -12,6 +12,7 @@
 STEP = 8
 EDGE = SPAN + WIN
 FAR = 3
+PUT_OFF = 1
 MESH = pl.DeviceIdType.MESH
 F32 = jnp.float32
 BF16 = jnp.bfloat16
@@ -26,17 +27,17 @@
 
 
 def kernel(
-    n_rx, n_ta, n_af, subs, pair,
+    n_rx, n_ta, n_af, subs, pair, put_off,
     traces_hbm, slopes_hbm, offsets_hbm, live_hbm,
     stack_ref, coherence_ref, peak_ref,
     slopes_ref, offsets_ref, live_ref,
-    held, delays, coming, long, left, total, edge_in, top, top_in,
+    held, coming, full, early, late, total, edge_in, top, top_in,
     in_sem, small_sem, gather_recv, right_send, left_send, far_send, far_ready,
     edge_send, edge_recv, top_send, top_recv,
 ):
     blocks = n_ta * n_af
     sub_rows, block_len = held.shape[2:]
-    own_slows = delays.shape[1]
+    own_slows = coming.shape[1]
     tall = block_len + STEP
     rx = lax.axis_index("rx")
     block = lax.axis_index("ta") * n_af + lax.axis_index("af")
@@ -106,8 +107,9 @@
         )
 
     total[...] = jnp.zeros_like(total)
-    long[0:STEP] = jnp.zeros((STEP, sub_rows), F32)
-    long[block_len + STEP:] = jnp.zeros((STEP, sub_rows), F32)
+    for _, long, _ in (full, early, late):
+        long[0:STEP] = jnp.zeros((STEP, sub_rows), F32)
+        long[block_len + STEP:] = jnp.zeros((STEP, sub_rows), F32)
 
     @pl.when(jnp.logical_not(has_next))
     def _():
@@ -167,45 +169,10 @@
         mine = number < subs
         return jnp.where(mine, rx, rx + distance), jnp.where(mine, number, sub)
 
+    far_count = jnp.maximum(n_rx - FAR - rx, 0)
+
     def exchange(sub):
-        before = jnp.maximum(rx - 1, 0)
-        after = jnp.minimum(rx + 1, n_rx - 1)
-
-        @pl.when(has_left)
-        def _():
-            to_right(before, sub).wait_recv()
-
-            @pl.when(has_right)
-            def _():
-                to_right(before, sub).start()
-
-        @pl.when(has_right)
-        def _():
-            to_left(after, sub).wait_recv()
-
-            @pl.when(has_left)
-            def _():
-                to_left(after, sub).start()
-
-    far_count = jnp.maximum(n_rx - FAR - rx, 0)
-
-    def add_item(number, carry):
-        source, sub = item_at(number)
-
-        pace = jnp.where(both > 0, 2, 1)
-        turn = lax.div(number - subs, pace)
-
-        @pl.when(jnp.logical_and(
-            number >= subs,
-            jnp.logical_and(turn < subs, lax.rem(number - subs, pace) == 0)))
-        def _():
-            exchange(turn)
-
-        @pl.when(jnp.abs(source - rx) > 1)
-        def _():
-            to_right(source, sub).wait_recv()
-
-        @pl.when(jnp.logical_and(number == 1, far_count > 0))
+        @pl.when(jnp.logical_and(sub == 0, far_count > 0))
         def _():
             pl.semaphore_wait(far_ready, far_count)
             for reach in range(FAR, n_rx):
@@ -214,13 +181,55 @@
                     for far_sub in range(subs):
                         to_far(jnp.minimum(rx + reach, n_rx - 1), far_sub).start()
 
+        before = jnp.maximum(rx - 1, 0)
+        after = jnp.minimum(rx + 1, n_rx - 1)
+
+        @pl.when(has_left)
+        def _():
+            to_right(before, sub).wait_recv()
+
+            @pl.when(has_right)
+            def _():
+                to_right(before, sub).start()
+
+        @pl.when(has_right)
+        def _():
+            to_left(after, sub).wait_recv()
+
+            @pl.when(has_left)
+            def _():
+                to_left(after, sub).start()
+
+    def await_item(number, source, sub):
+        pace = jnp.where(both > 0, 2, 1)
+        ahead = number - subs
+        turn = jnp.where(both > 0, lax.div(ahead, 2), ahead)
+
+        @pl.when(jnp.logical_and(
+            number >= subs, jnp.logical_and(turn < subs, turn * pace == ahead)))
+        def _():
+            exchange(turn)
+
+        @pl.when(jnp.abs(source - rx) > 1)
+        def _():
+            to_right(source, sub).wait_recv()
+
+    last = n_rx * subs - 1
+
+    def add_rows(number, place, rows, buffers, arriving):
+        low, high = rows
+        size = high - low
+        delays, long, left = buffers
+        source, sub = place
+        if arriving:
+            await_item(number, source, sub)
         delays[...] = coming[...]
         long[STEP:STEP + block_len] = held[source, sub].astype(F32).T
-        delay = delays[...]
         for lag in range(STEP):
-            samples = long[lag:lag + tall]
+            samples = long[lag + low:lag + high]
             left[:, lag * sub_rows:(lag + 1) * sub_rows] = jnp.concatenate(
                 [samples, samples * samples], axis=0).astype(BF16)
+        delay = delays[...]
         for first in range(0, SPAN // STEP, pair):
             right = [
                 jnp.concatenate([
@@ -232,16 +241,32 @@
             product = jnp.dot(left[...], jnp.concatenate(right, axis=0),
                               preferred_element_type=F32)
             for turn in range(pair):
-                top_row = SPAN - STEP * (first + turn + 1)
+                shift = SPAN - STEP * (first + turn + 1)
                 lanes = slice(turn * own_slows, (turn + 1) * own_slows)
-                total[0, top_row:top_row + tall] += product[:tall, lanes]
-                total[1, top_row:top_row + tall] += product[tall:, lanes]
-        coming[...] = delays_of(*item_at(jnp.minimum(number + 1, n_rx * subs - 1)))
-        return carry
+                total[0, shift + low:shift + high] += product[:size, lanes]
+                total[1, shift + low:shift + high] += product[size:, lanes]
+
+    def add_full(number, place):
+        add_rows(number, place, (0, tall), full, True)
+        following = item_at(number + 1)
+        coming[...] = delays_of(*following)
+        return following
+
+    def add_early(number, place):
+        add_rows(number, place, (0, EDGE), early, True)
+        following = item_at(jnp.where(number == last, last + 1 - put_off, number + 1))
+        coming[...] = delays_of(*following)
+        return following
+
+    def add_late(number, place):
+        add_rows(number, place, (EDGE, tall), late, False)
+        following = item_at(jnp.minimum(number + 1, last))
+        coming[...] = delays_of(*following)
+        return following
 
     coming[...] = delays_of(rx, 0)
-
-    lax.fori_loop(0, n_rx * subs, add_item, 0)
+    place = lax.fori_loop(0, last + 1 - put_off, add_full, (rx, jnp.int32(0)))
+    place = lax.fori_loop(last + 1 - put_off, last + 1, add_early, place)
 
     pass_edge = pltpu.make_async_remote_copy(
         src_ref=total.at[:, pl.ds(0, EDGE)], dst_ref=edge_in,
@@ -252,6 +277,8 @@
     @pl.when(has_previous)
     def _():
         pass_edge.start()
+
+    lax.fori_loop(last + 1 - put_off, last + 1, add_late, place)
 
     @pl.when(has_next)
     def _():
@@ -341,6 +368,15 @@
         pair = min(max(256 // own_slows, 1), SPAN // STEP)
         blocks = n_ta * n_af
         tall = block_len + STEP
+        put_off = min(PUT_OFF, n_rx * subs - 1)
+
+        def working(rows):
+            return (
+                pltpu.VMEM((sub_rows, own_slows), BF16),
+                pltpu.VMEM((block_len + 2 * STEP, sub_rows), F32),
+                pltpu.VMEM((2 * rows, STEP * sub_rows), BF16),
+            )
+
         dma = pltpu.SemaphoreType.DMA
         vmem = pl.BlockSpec(memory_space=pltpu.VMEM)
         anywhere = pl.BlockSpec(memory_space=pl.ANY)
@@ -350,7 +386,7 @@
             jax.ShapeDtypeStruct((1, own_slows), F32),
         )
         results = pl.pallas_call(
-            functools.partial(kernel, n_rx, n_ta, n_af, subs, pair),
+            functools.partial(kernel, n_rx, n_ta, n_af, subs, pair, put_off),
             out_shape=shapes,
             in_specs=[pl.BlockSpec(memory_space=pltpu.HBM)] * 4,
             out_specs=(vmem,) * 3,
@@ -360,9 +396,7 @@
                 pltpu.VMEM((1, n_rx * local_rows), jnp.int32),
                 pltpu.VMEM((n_rx, subs, sub_rows, block_len), BF16),
                 pltpu.VMEM((sub_rows, own_slows), BF16),
-                pltpu.VMEM((sub_rows, own_slows), BF16),
-                pltpu.VMEM((block_len + 2 * STEP, sub_rows), F32),
-                pltpu.VMEM((2 * tall, STEP * sub_rows), BF16),
+                working(tall), working(EDGE), working(tall - EDGE),
                 pltpu.VMEM((2, block_len + SPAN, own_slows), F32),
                 pltpu.VMEM((2, EDGE, own_slows), F32),
                 pltpu.VMEM((1, own_slows), F32),

time: 23.1 us -> 22.8 us (0.987)
  Pallas kernels: 22.3 us -> 22 us
    pallas_call x1, Pallas kernels: 21.6 us -> 21.3 us  [on_device(): pl.pallas_call(functools.partial(kernel, n_rx, n_ta, n_af, subs, pair, pu...]
where the time goes in v3:
time: 22.8 us; the launch traced here: 22.6 us
  Pallas kernels  22 us (96%)
  between operations  0.64 us (3%)
    pallas_call x1, Pallas kernels, on_device(): pl.pallas_call(functools.partial(kernel, n_rx, n_ta, n_af, subs, pair, pu...  21.3 us
    pallas_call x1, Pallas kernels, on_device(): pl.pallas_call(emit, out_shape=shapes, in_specs=[vmem] * 3, out_specs=(an...  0.68 us

profile of v3, /device:TPU:0, one launch (start us, length us, event | category | flops | bytes accessed | tf_op | source)
XLA Modules:
  0.0 22.6 jit_solution(10330960374497648067)
XLA Ops:
  0.6 21.3 %slant_stack.1 = (f32[128,128]{1,0:T(8,128)S(1)}, f32[128,128]{1,0:T(8,128)S(1)}, f32[1,128]{1,0:T(1,128)S(1)}) custom-call(bf16[512,128]{1,0:T(8,128)(2,1)} %traces_hbm.1, s32[4,128]{1,0:T(4,128)} %bitcast.6, s32[1,2048]{1,0:T(1,128)} %bitcast.4, s32[1,2048]{1,0:T(1,128)} %bitcast.5), custom_call_target="tpu_custom_call" | custom-call | tf_op jit(solution)/shard_map/slant_stack/pallas_call | solution.py:388
  21.9 0.7 %emit.1 = (f32[128,128]{1,0:T(8,128)}, f32[128,128]{1,0:T(8,128)}, f32[1,128]{1,0:T(1,128)}) custom-call(f32[128,128]{1,0:T(8,128)S(1)} %get-tuple-element.9.stack_ref, f32[128,128]{1,0:T(8,128)S(1)} %get-tuple-element.10.coherence_ref, f32[1,128]{1,0:T(1,128)S(1)} %get-tuple-element.11.peak_ref), custom_call_target="tpu_custom_call" | custom-call | tf_op jit(solution)/shard_map/emit/pallas_call | solution.py:412

commit v4 on v3

--- a/solution.py
+++ b/solution.py
@@ -127,9 +127,10 @@
         def _():
             to_right(rx, sub).start()
 
-        @pl.when(has_left)
-        def _():
-            to_left(rx, sub).start()
+        if sub == 0:
+            @pl.when(has_left)
+            def _():
+                to_left(rx, 0).start()
 
         for reach in range(FAR, n_rx):
             @pl.when(rx >= reach)
@@ -139,6 +140,11 @@
                 if sub == 0:
                     pl.semaphore_signal(
                         far_ready, inc=1, device_id={"rx": target}, device_id_type=MESH)
+
+    for sub in range(1, subs):
+        @pl.when(has_left)
+        def _():
+            to_left(rx, sub).start()
 
     slopes = slopes_ref[pl.ds(rx, 1), :].astype(F32)
 
@@ -171,7 +177,7 @@
 
     far_count = jnp.maximum(n_rx - FAR - rx, 0)
 
-    def exchange(sub):
+    def exchange(sub, whole):
         @pl.when(jnp.logical_and(sub == 0, far_count > 0))
         def _():
             pl.semaphore_wait(far_ready, far_count)
@@ -192,7 +198,7 @@
             def _():
                 to_right(before, sub).start()
 
-        @pl.when(has_right)
+        @pl.when(jnp.logical_and(has_right, jnp.logical_or(whole, sub > 0)))
         def _():
             to_left(after, sub).wait_recv()
 
@@ -208,7 +214,13 @@
         @pl.when(jnp.logical_and(
             number >= subs, jnp.logical_and(turn < subs, turn * pace == ahead)))
         def _():
-            exchange(turn)
+            exchange(turn, both == 0)
+
+        @pl.when(jnp.logical_and(both > 0, ahead == 1))
+        def _():
+            after = jnp.minimum(rx + 1, n_rx - 1)
+            to_left(after, 0).wait_recv()
+            to_left(after, 0).start()
 
         @pl.when(jnp.abs(source - rx) > 1)
         def _():

time: 22.8 us -> 22.6 us (level)
  no operation moved by 1% of the time
where the time goes in v4:
time: 22.6 us; the launch traced here: 22.4 us
  Pallas kernels  21.8 us (96%)
  between operations  0.64 us (3%)
    pallas_call x1, Pallas kernels, on_device(): pl.pallas_call(functools.partial(kernel, n_rx, n_ta, n_af, subs, pair, pu...  21.1 us
    pallas_call x1, Pallas kernels, on_device(): pl.pallas_call(emit, out_shape=shapes, in_specs=[vmem] * 3, out_specs=(an...  0.68 us

profile of v4, /device:TPU:0, one launch (start us, length us, event | category | flops | bytes accessed | tf_op | source)
XLA Modules:
  0.0 22.4 jit_solution(1552646402208923366)
XLA Ops:
  0.6 21.1 %slant_stack.1 = (f32[128,128]{1,0:T(8,128)S(1)}, f32[128,128]{1,0:T(8,128)S(1)}, f32[1,128]{1,0:T(1,128)S(1)}) custom-call(bf16[512,128]{1,0:T(8,128)(2,1)} %traces_hbm.1, s32[4,128]{1,0:T(4,128)} %bitcast.6, s32[1,2048]{1,0:T(1,128)} %bitcast.4, s32[1,2048]{1,0:T(1,128)} %bitcast.5), custom_call_target="tpu_custom_call" | custom-call | tf_op jit(solution)/shard_map/slant_stack/pallas_call | solution.py:400
  21.8 0.7 %emit.1 = (f32[128,128]{1,0:T(8,128)}, f32[128,128]{1,0:T(8,128)}, f32[1,128]{1,0:T(1,128)}) custom-call(f32[128,128]{1,0:T(8,128)S(1)} %get-tuple-element.9.stack_ref, f32[128,128]{1,0:T(8,128)S(1)} %get-tuple-element.10.coherence_ref, f32[1,128]{1,0:T(1,128)S(1)} %get-tuple-element.11.peak_ref), custom_call_target="tpu_custom_call" | custom-call | tf_op jit(solution)/shard_map/emit/pallas_call | solution.py:424

commit v5 on v4

--- a/solution.py
+++ b/solution.py
@@ -27,7 +27,7 @@
 
 
 def kernel(
-    n_rx, n_ta, n_af, subs, pair, put_off,
+    n_rx, n_ta, n_af, subs, pair, most_put_off,
     traces_hbm, slopes_hbm, offsets_hbm, live_hbm,
     stack_ref, coherence_ref, peak_ref,
     slopes_ref, offsets_ref, live_ref,
@@ -227,6 +227,8 @@
             to_right(source, sub).wait_recv()
 
     last = n_rx * subs - 1
+    crossing = jnp.logical_and(has_previous, lax.axis_index("af") == 0)
+    put_off = jnp.where(crossing, most_put_off, 0)
 
     def add_rows(number, place, rows, buffers, arriving):
         low, high = rows
@@ -260,7 +262,7 @@
 
     def add_full(number, place):
         add_rows(number, place, (0, tall), full, True)
-        following = item_at(number + 1)
+        following = item_at(jnp.minimum(number + 1, last))
         coming[...] = delays_of(*following)
         return following
 
@@ -280,35 +282,47 @@
     place = lax.fori_loop(0, last + 1 - put_off, add_full, (rx, jnp.int32(0)))
     place = lax.fori_loop(last + 1 - put_off, last + 1, add_early, place)
 
-    pass_edge = pltpu.make_async_remote_copy(
-        src_ref=total.at[:, pl.ds(0, EDGE)], dst_ref=edge_in,
-        send_sem=edge_send, recv_sem=edge_recv,
-        device_id=previous, device_id_type=MESH,
-    )
+    def pass_edge(kind):
+        return pltpu.make_async_remote_copy(
+            src_ref=total.at[kind, pl.ds(0, EDGE)], dst_ref=edge_in.at[kind],
+            send_sem=edge_send.at[kind], recv_sem=edge_recv.at[kind],
+            device_id=previous, device_id_type=MESH,
+        )
 
     @pl.when(has_previous)
     def _():
-        pass_edge.start()
+        for kind in range(2):
+            pass_edge(kind).start()
 
     lax.fori_loop(last + 1 - put_off, last + 1, add_late, place)
 
-    @pl.when(has_next)
-    def _():
-        pass_edge.wait_recv()
-
     near_rows = block_len - SPAN
-
-    def whole(kind):
+    sure = near_rows - WIN
+
+    def near(kind):
+        return total[kind, SPAN:block_len]
+
+    def far(kind):
+        @pl.when(has_next)
+        def _():
+            pass_edge(kind).wait_recv()
+
         return jnp.concatenate([
-            total[kind, SPAN:SPAN + near_rows],
-            total[kind, SPAN + near_rows:] + edge_in[kind, 0:SPAN],
+            total[kind, SPAN + sure:block_len],
+            total[kind, block_len:] + edge_in[kind, 0:SPAN],
             edge_in[kind, SPAN:],
         ], axis=0)
 
-    stack, energy = whole(0), whole(1)
-    power_sum = window_sum(stack * stack, WIN)[:block_len]
-    energy_sum = window_sum(energy, WIN)[:block_len]
-    coherence = power_sum / jnp.maximum(energy_sum, 1.0)
+    def windows(rows):
+        return window_sum(rows, WIN)[:rows.shape[0] - WIN]
+
+    near_stack = near(0)
+    near_coherence = windows(near_stack * near_stack) / jnp.maximum(windows(near(1)), 1.0)
+    far_stack = far(0)
+    far_power = windows(far_stack * far_stack)
+    far_coherence = far_power / jnp.maximum(windows(far(1)), 1.0)
+    stack = jnp.concatenate([near_stack[:sure], far_stack], axis=0)
+    coherence = jnp.concatenate([near_coherence, far_coherence], axis=0)
     peak = jnp.max(coherence, axis=0, keepdims=True)
     top[...] = peak
     tops = []
@@ -347,7 +361,8 @@
 
     @pl.when(has_previous)
     def _():
-        pass_edge.wait_send()
+        for kind in range(2):
+            pass_edge(kind).wait_send()
 
     for step, copy in enumerate(tops):
         copy.wait_recv()
@@ -415,7 +430,7 @@
                 pltpu.VMEM((max(blocks - 1, 1), 1, own_slows), F32),
                 dma((subs,)), dma((3,)), dma((n_rx, subs)), dma((n_rx, subs)), dma((n_rx, subs)),
                 dma((n_rx, subs)), pltpu.SemaphoreType.REGULAR,
-                dma, dma,
+                dma((2,)), dma((2,)),
                 dma((max(blocks - 1, 1),)), dma((max(blocks - 1, 1),)),
             ],
             compiler_params=pltpu.CompilerParams(collective_id=0, has_side_effects=True, vmem_limit_bytes=16777216),

time: 22.6 us -> 22.6 us (level)
  no operation moved by 1% of the time
where the time goes in v5:
time: 22.6 us; the launch traced here: 22.4 us
  Pallas kernels  21.8 us (96%)
  between operations  0.64 us (3%)
    pallas_call x1, Pallas kernels, on_device(): pl.pallas_call(functools.partial(kernel, n_rx, n_ta, n_af, subs, pair, pu...  21.1 us
    pallas_call x1, Pallas kernels, on_device(): pl.pallas_call(emit, out_shape=shapes, in_specs=[vmem] * 3, out_specs=(an...  0.68 us

profile of v5, /device:TPU:0, one launch (start us, length us, event | category | flops | bytes accessed | tf_op | source)
XLA Modules:
  0.0 22.4 jit_solution(1165072029379588533)
XLA Ops:
  0.6 21.1 %slant_stack.1 = (f32[128,128]{1,0:T(8,128)S(1)}, f32[128,128]{1,0:T(8,128)S(1)}, f32[1,128]{1,0:T(1,128)S(1)}) custom-call(bf16[512,128]{1,0:T(8,128)(2,1)} %traces_hbm.1, s32[4,128]{1,0:T(4,128)} %bitcast.6, s32[1,2048]{1,0:T(1,128)} %bitcast.4, s32[1,2048]{1,0:T(1,128)} %bitcast.5), custom_call_target="tpu_custom_call" | custom-call | tf_op jit(solution)/shard_map/slant_stack/pallas_call | solution.py:415
  21.7 0.7 %emit.1 = (f32[128,128]{1,0:T(8,128)}, f32[128,128]{1,0:T(8,128)}, f32[1,128]{1,0:T(1,128)}) custom-call(f32[128,128]{1,0:T(8,128)S(1)} %get-tuple-element.9.stack_ref, f32[128,128]{1,0:T(8,128)S(1)} %get-tuple-element.10.coherence_ref, f32[1,128]{1,0:T(1,128)S(1)} %get-tuple-element.11.peak_ref), custom_call_target="tpu_custom_call" | custom-call | tf_op jit(solution)/shard_map/emit/pallas_call | solution.py:439
